TPU v7x, 16 devices: a whole 2x2x2 slice. The times are simulated.
16 devices in a mesh: dp: 2 (over z), vp: 8 (over y, x, core).
Axes of the slice: x: 2, y: 2, z: 2, core: 2. Of those that a mesh axis runs over, the one named last changes fastest.
Arguments:
- hidden: bfloat16 [2048, 512], P('dp')
- norm_scale: float32 [512], replicated
- w_out: bfloat16 [512, 250112], P(None, 'vp')
- targets: int32 [2048], P('dp')
- weights: float32 [2048], P('dp')
Outputs:
- output 1: float32 [], replicated
- output 2: bfloat16 [2048, 512], P('dp')
- output 3: float32 [512, 250112], P(None, 'vp')
- output 4: float32 [512], replicated
All inputs are finite; a program needn't handle non-finite values.
Results may differ from a plain program's by a relative error of at most 0.001.
Values sent between devices are 32-bit elements.
A program may use at most 1 GiB of HBM per device.

v0:
```python
import jax
import jax.numpy as jnp
from jax import lax
from jax.sharding import PartitionSpec as P

EPS = 1e-6


def rms_norm(h_float, norm_scale):
    mean_sq = jnp.mean(h_float * h_float, axis=-1, keepdims=True)
    return h_float * lax.rsqrt(mean_sq + EPS) * norm_scale


def solution(mesh):
    def local(h_loc, norm_scale, w_loc, tgt_loc, wt_loc):
        vocab_loc = w_loc.shape[1]
        offset = lax.axis_index('vp') * vocab_loc
        w_total = lax.psum(jnp.sum(wt_loc), 'dp')
        normed, norm_vjp = jax.vjp(rms_norm, h_loc.astype(jnp.float32), norm_scale)
        h_norm = normed.astype(jnp.bfloat16)
        logits = jnp.dot(h_norm, w_loc, preferred_element_type=jnp.float32)
        row_max = lax.pmax(jnp.max(logits, axis=-1, keepdims=True), 'vp')
        exp_shift = jnp.exp(logits - row_max)
        sum_exp = lax.psum(jnp.sum(exp_shift, axis=-1, keepdims=True), 'vp')
        log_norm = row_max[:, 0] + jnp.log(sum_exp[:, 0])
        vocab_ids = lax.broadcasted_iota(jnp.int32, (1, vocab_loc), 1) + offset
        is_target = vocab_ids == tgt_loc[:, None]
        tgt_logit = lax.psum(jnp.sum(jnp.where(is_target, logits, 0.0), axis=-1), 'vp')
        loss = lax.psum(jnp.sum(wt_loc * (log_norm - tgt_logit)), 'dp') / w_total
        tok_coef = (wt_loc / w_total)[:, None]
        grad_logits = ((tok_coef / sum_exp) * exp_shift - jnp.where(is_target, tok_coef, 0.0)).astype(jnp.bfloat16)
        grad_hn = lax.psum(lax.dot_general(grad_logits, w_loc, (((1,), (1,)), ((), ())), preferred_element_type=jnp.float32), 'vp')
        grad_w = lax.psum(lax.dot_general(h_norm, grad_logits, (((0,), (0,)), ((), ())), preferred_element_type=jnp.float32), 'dp')
        grad_h, grad_scale = norm_vjp(grad_hn)
        return loss, grad_h.astype(jnp.bfloat16), grad_w, lax.psum(grad_scale, 'dp')

    return jax.shard_map(local, mesh=mesh, in_specs=(P('dp', None), P(None), P(None, 'vp'), P('dp'), P('dp')), out_specs=(P(), P('dp', None), P(None, 'vp'), P(None)), check_vma=False)
```

profile of v0, /device:TPU:0, one launch (start us, length us, event | category | flops | bytes accessed | tf_op | source)
XLA Modules:
  0.0 1737.8 jit_solution(3742836072181176457)
XLA Ops:
  7.2 0.0 all-reduce.5.cloned.1.call-start
  7.2 1.5 fusion.9
  8.7 0.0 copy-start.1
  8.7 0.6 copy-done.1
  9.3 0.0 copy-start.3
  9.3 58.0 %fusion.17 = (f32[1024]{0:T(1024)S(1)}, f32[1024,31264]{0,1:T(8,128)}) fusion(bf16[512,31264]{0,1:T(8,128)(2,1)} %param.7, bf16[1024,512]{1,0:T(8,128)(2,1)} %param.5, f32[512]{0:T(512)} %param.6, f32[1024]{0:T(1024)S(1)} %fusion.15), kind=kOutput, calls=%fused_computation.28 | convolution fusion | flops 32816791552 | bytes 161130496 | tf_op jit(solution)/shard_map/dot_general | solution.py:21
  67.3 15.4 pmax.7
  82.7 0.0 copy-done.3
  82.7 0.0 copy-start.4
  82.7 39.8 %fusion.3 = (f32[1024]{0:T(1024)S(1)}, f32[1024]{0:T(1024)S(1)}) fusion(f32[1024,31264]{0,1:T(8,128)} %get-tuple-element.15, f32[1024]{0:T(1024)S(1)} %pmax.7, s32[1024]{0:T(1024)S(1)} %copy-done.3, s32[31264]{0:T(1024)S(1)} %iota_add_fusion), kind=kLoop, calls=%fused_computation.6 | loop fusion | flops 160069632 | bytes 128198784 | tf_op jit(solution)/shard_map/reduce_sum | solution.py:24
  122.6 12.1 all-reduce
  134.7 0.0 copy-done.4
  134.7 0.6 fusion.16
  135.3 5.7 psum.52
  141.1 0.6 broadcast_divide_fusion
  141.7 61.8 %fusion.2 = bf16[1024,31264]{0,1:T(8,128)(2,1)} fusion(f32[1024,31264]{0,1:T(8,128)} %get-tuple-element.15, f32[1024]{0:T(1024)S(1)} %broadcast_divide_fusion, f32[1024]{0:T(1024)S(1)} %bitcast.11, s32[1024]{0:T(1024)S(1)} %copy-done.3, f32[1024]{0:T(1024)S(1)} %pmax.7, s32[31264]{0:T(1024)S(1)} %iota_add_fusion), kind=kLoop, calls=%fused_computation.4 | loop fusion | flops 192086016 | bytes 192227456 | tf_op jit(solution)/shard_map/convert_element_type | solution.py:31
  203.5 0.0 copy-start
  203.5 0.0 copy-start.5
  203.6 42.5 %fusion.18 = f32[1024,512]{1,0:T(8,128)} fusion(bf16[1024,31264]{0,1:T(8,128)(2,1)} %fusion.2, bf16[512,31264]{0,1:T(8,128)(2,1)} %param.7), kind=kOutput, calls=%fused_computation.29 | convolution fusion | flops 32782680064 | bytes 98140160 | tf_op jit(solution)/shard_map/dot_general | solution.py:32
  246.0 0.0 all-reduce.5.cloned.1.call-update
  246.0 0.3 all-reduce.7.cloned.1.call-start
  246.3 0.0 copy-done
  246.3 0.0 copy-done.5
  246.3 55.2 %fusion.11 = f32[512,31264]{0,1:T(8,128)} fusion(bf16[1024,31264]{0,1:T(8,128)(2,1)} %fusion.2, bf16[1024,512]{1,0:T(8,128)(2,1)S(1)} %copy-done, f32[512]{0:T(512)S(1)} %copy-done.5, f32[1024]{0:T(1024)S(1)} %fusion.15), kind=kOutput, calls=%fused_computation.19 | convolution fusion | flops 32784777216 | bytes 129112064 | tf_op jit(solution)/shard_map/dot_general | solution.py:33
  301.6 0.0 copy-start.2
  301.6 0.0 all-reduce.7.cloned.1.call-update
  301.6 0.0 all-reduce.5.cloned.1.call-done
  301.6 2.4 fusion.7
  304.1 5.6 all-reduce.1
  311.0 0.0 copy-done.2
  311.0 3.1 fusion.8
  314.1 1373.6 %all-reduce.7.cloned.1.call-done = f32[512,31264]{0,1:T(8,128)} async-done(((f32[512,31264]{0,1:T(8,128)}), f32[512,31264]{0,1:T(8,128)}) %all-reduce.7.cloned.1.call-update) | async-done | bytes 64028688 | tf_op jit(solution)/shard_map/psum | solution.py:33
  1687.6 42.2 %copy.11 = f32[512,31264]{0,1:T(8,128)} copy(f32[512,31264]{0,1:T(8,128)} %all-reduce.7.cloned.1.call-done) | data formatting | bytes 128057344
  (5 shorter events, 0.1 us)
Async XLA Ops:
  7.2 294.4 %all-reduce.5.cloned.1.call-start = ((), (), s32[]{:S(2)}) async-start(), calls=%async_computation | async-start | bytes 4194304 | tf_op jit(solution)/shard_map/psum | solution.py:32
  8.7 0.6 copy-start.1
  9.3 73.4 %copy-start.3 = (s32[1024]{0:T(1024)S(1)}, s32[1024]{0:T(1024)}, u32[]{:S(2)}) copy-start(s32[1024]{0:T(1024)} %param.8) | copy-start | bytes 12292
  82.7 52.0 %copy-start.4 = (f32[1024]{0:T(1024)S(1)}, f32[1024]{0:T(1024)}, u32[]{:S(2)}) copy-start(f32[1024]{0:T(1024)} %param.9) | copy-start | bytes 12292
  203.5 42.8 %copy-start = (bf16[1024,512]{1,0:T(8,128)(2,1)S(1)}, bf16[1024,512]{1,0:T(8,128)(2,1)}, u32[]{:S(2)}) copy-start(bf16[1024,512]{1,0:T(8,128)(2,1)} %param.5) | copy-start | bytes 3145732
  203.5 42.8 %copy-start.5 = (f32[512]{0:T(512)S(1)}, f32[512]{0:T(512)}, u32[]{:S(2)}) copy-start(f32[512]{0:T(512)} %param.6) | copy-start | bytes 6148
  246.0 1441.6 %all-reduce.7.cloned.1.call-start = ((), (), s32[]{:S(2)}) async-start(), calls=%async_computation.1 | async-start | bytes 128057344 | tf_op jit(solution)/shard_map/psum | solution.py:33
  301.6 9.4 copy-start.2
Sparse Core Ops, SparseCore 0:
  246.2 52.8 all-reduce.4
  301.7 1385.8 all-reduce.6
where the time goes:
time: 1740 us
  waiting for transfers between devices  1370 us (79%)
  matrix products  156 us (9%)
  other arithmetic  110 us (6%)
  local copies, waits for them, and re-layouts  42.8 us (2%)
  blocking collectives  38.8 us (2%)
    psum x1, waiting for transfers between devices, local(): lax.psum(lax.dot_general(h_norm, grad_logits, (((0,), (0,)), ((), ())), p...  1370 us
    convert_element_type x1, other arithmetic, local(): (tok_coef / sum_exp * exp_shift - jnp.where(is_target, tok_coef, 0.0)).as...  61.8 us
    dot_general x1, matrix products, local(): logits = jnp.dot(h_norm, w_loc, preferred_element_type=jnp.float32)  58 us
    dot_general x1, matrix products, local(): lax.dot_general(h_norm, grad_logits, (((0,), (0,)), ((), ())), preferred_...  55.2 us
    unnamed x13, local copies, waits for them, and re-layouts  42.8 us
    dot_general x1, matrix products, local(): lax.dot_general(grad_logits, w_loc, (((1,), (1,)), ((), ())), preferred_e...  42.5 us
    reduce_sum x1, other arithmetic, local(): sum_exp = lax.psum(jnp.sum(exp_shift, axis=-1, keepdims=True), 'vp')  39.8 us
  transfers between devices with their start and end apart: 2, of which 1 were waited for; matrix products, arithmetic and copies ran while one was open for 3% of the time, Pallas kernels for 0%

commit v1 on v0

v1 whole, which is shorter than its diff:
```python
import functools

import jax
import jax.numpy as jnp
from jax import lax
from jax.experimental import pallas as pl
from jax.experimental.pallas import tpu as pltpu
from jax.sharding import PartitionSpec as P

EPS = 1e-6
SUB = 8
BLOCK_V = 768
CHUNK = 512
GROUP = 64
FIRST = 22
TN = (((0,), (0,)), ((), ()))


def stats_kernel(vocab, hnt_ref, w_ref, out_ref, m_ref, s_ref):
    i = pl.program_id(0)
    last = pl.num_programs(0) - 1
    tokens = hnt_ref.shape[1]

    @pl.when(i == 0)
    def _():
        m_ref[...] = jnp.full(m_ref.shape, -jnp.inf, jnp.float32)
        s_ref[...] = jnp.zeros(s_ref.shape, jnp.float32)

    def block(rows):
        for c in range(0, tokens, CHUNK):
            cols = pl.ds(c, CHUNK)
            z = jnp.dot(w_ref[:rows, :], hnt_ref[:, cols], preferred_element_type=jnp.float32)
            m, s = m_ref[:, cols], s_ref[:, cols]
            for r in range(0, rows, GROUP):
                n = min(GROUP, rows - r)
                part = z[r:r + n].reshape(n // SUB, SUB, CHUNK)
                m_new = jnp.maximum(m, jnp.max(part, axis=0))
                s = s * jnp.exp(m - m_new) + jnp.sum(jnp.exp(part - m_new[None]), axis=0)
                m = m_new
            m_ref[:, cols] = m
            s_ref[:, cols] = s

    @pl.when(i < last)
    def _():
        block(BLOCK_V)

    @pl.when(i == last)
    def _():
        block(vocab - (vocab - 1) // BLOCK_V * BLOCK_V)
        top = jnp.max(m_ref[...], axis=0, keepdims=True)
        out_ref[0:1, :] = top
        out_ref[1:2, :] = jnp.sum(s_ref[...] * jnp.exp(m_ref[...] - top), axis=0, keepdims=True)


def zero_tail(vocab, w_ref, wz_ref, is_last):
    tail = vocab - (vocab - 1) // BLOCK_V * BLOCK_V
    wz_ref[...] = w_ref[...]

    @pl.when(is_last)
    def _():
        wz_ref[tail:, :] = jnp.zeros((BLOCK_V - tail, wz_ref.shape[1]), jnp.bfloat16)


def softmax_grad(step, wz_ref, hnt_ref, tok_ref, base, g_ref, zt_ref=None):
    shape = (BLOCK_V // SUB, SUB, CHUNK)
    first_row = (lax.broadcasted_iota(jnp.int32, shape, 0) * SUB).astype(jnp.float32)
    sub = lax.broadcasted_iota(jnp.int32, shape[1:], 0)
    row0 = (sub + step * BLOCK_V).astype(jnp.float32)
    for c in range(0, hnt_ref.shape[1], CHUNK):
        cols, toks = pl.ds(c, CHUNK), pl.ds(base + c, CHUNK)
        z = jnp.dot(wz_ref[...], hnt_ref[:, cols], preferred_element_type=jnp.float32).reshape(shape)
        hit = (tok_ref[2 * SUB:, toks] - row0)[None] == first_row
        g = jnp.exp(z - tok_ref[:SUB, toks][None]) - jnp.where(hit, tok_ref[SUB:2 * SUB, toks][None], 0.0)
        g_ref[:, cols] = g.reshape(BLOCK_V, CHUNK).astype(jnp.bfloat16)
        if zt_ref is not None:
            zt_ref[:, cols] += jnp.sum(jnp.where(hit, z, 0.0), axis=0)


def first_kernel(vocab, hn_a_ref, hn_b_ref, hnt_a_ref, hnt_b_ref, w_ref, tok_ref, dw_ref, x_ref, g_out_ref, wz_ref, ga_ref, gb_ref):
    i = pl.program_id(0)
    width, own = hnt_a_ref.shape
    dhnt_ref = x_ref.at[:width]
    zt_ref = x_ref.at[width:]

    @pl.when(i == 0)
    def _():
        x_ref[...] = jnp.zeros(x_ref.shape, jnp.float32)

    zero_tail(vocab, w_ref, wz_ref, i == pl.num_programs(0) - 1)

    def own_part(g_ref):
        softmax_grad(i, wz_ref, hnt_a_ref, tok_ref, 0, g_ref, zt_ref)
        dhnt_ref[...] += lax.dot_general(wz_ref[...], g_ref[...], TN, preferred_element_type=jnp.float32)

    @pl.when(i < FIRST)
    def _():
        own_part(ga_ref)
        softmax_grad(i, wz_ref, hnt_b_ref, tok_ref, own, gb_ref)
        dw_ref[...] = jnp.dot(ga_ref[...], hn_a_ref[...], preferred_element_type=jnp.float32) + jnp.dot(gb_ref[...], hn_b_ref[...], preferred_element_type=jnp.float32)

    @pl.when(i >= FIRST)
    def _():
        own_part(g_out_ref)


def second_kernel(vocab, hn_a_ref, hn_b_ref, hnt_b_ref, w_ref, tok_ref, g_in_ref, dw_in_ref, dw_ref, wz_ref, gb_ref):
    i = pl.program_id(0)
    own = hnt_b_ref.shape[1]
    zero_tail(vocab, w_ref, wz_ref, i == pl.num_programs(0) - 1)
    softmax_grad(i + FIRST, wz_ref, hnt_b_ref, tok_ref, own, gb_ref)
    dw_ref[...] = jnp.dot(g_in_ref[...], hn_a_ref[...], preferred_element_type=jnp.float32) + jnp.dot(gb_ref[...], hn_b_ref[...], preferred_element_type=jnp.float32)


def full(shape):
    return pl.BlockSpec(shape, lambda i: (0,) * len(shape))


def solution(mesh):
    dp, vp = mesh.shape['dp'], mesh.shape['vp']

    def local(h_loc, norm_scale, w_loc, tgt_loc, wt_loc):
        own, width = h_loc.shape
        vocab = w_loc.shape[1]
        tokens = dp * own
        steps = pl.cdiv(vocab, BLOCK_V)
        me = lax.axis_index('vp')
        my_dp = lax.axis_index('dp')
        swap_dp = [(0, 1), (1, 0)]
        w_t = w_loc.T

        h_own = h_loc.astype(jnp.float32)
        h_oth = lax.ppermute(h_own, 'dp', swap_dp)
        tgt_oth = lax.ppermute(tgt_loc, 'dp', swap_dp)
        wt_oth = lax.ppermute(wt_loc, 'dp', swap_dp)

        def rstd(h):
            return lax.rsqrt(jnp.mean(h * h, axis=-1, keepdims=True) + EPS)

        r_own = rstd(h_own)
        hn_own = (h_own * r_own * norm_scale).astype(jnp.bfloat16)
        hnt_own = hn_own.T

        params = pltpu.CompilerParams(dimension_semantics=('arbitrary',), vmem_limit_bytes=60 * 2**20)
        unit = 2 * own * width * vocab
        st = pl.pallas_call(
            functools.partial(stats_kernel, vocab),
            grid=(steps,),
            in_specs=[full((width, own)), pl.BlockSpec((BLOCK_V, width), lambda i: (i, 0))],
            out_specs=full((2, own)),
            out_shape=jax.ShapeDtypeStruct((2, own), jnp.float32),
            scratch_shapes=[pltpu.VMEM((SUB, own), jnp.float32)] * 2,
            compiler_params=params,
            cost_estimate=pl.CostEstimate(flops=unit, bytes_accessed=2 * width * vocab, transcendentals=own * vocab),
            name='stats',
        )(hnt_own, w_t)
        h_oth, tgt_oth, wt_oth, st = lax.optimization_barrier((h_oth, tgt_oth, wt_oth, st))
        stats = lax.all_gather(st, ('dp', 'vp')).reshape(dp, vp, 2, own)
        top = jnp.max(stats[:, :, 0], axis=1)
        log_norm = top + jnp.log(jnp.sum(stats[:, :, 1] * jnp.exp(stats[:, :, 0] - top[:, None]), axis=1))
        w_total = jnp.sum(wt_loc) + jnp.sum(wt_oth)
        log_own = lax.dynamic_index_in_dim(log_norm, my_dp, 0, keepdims=False)
        log_oth = lax.dynamic_index_in_dim(log_norm, 1 - my_dp, 0, keepdims=False)

        hn_oth = (h_oth * rstd(h_oth) * norm_scale).astype(jnp.bfloat16)
        hnt_oth = hn_oth.T
        coef = jnp.concatenate([wt_loc, wt_oth]) / w_total
        lp = jnp.concatenate([log_own, log_oth]) - jnp.log(coef)
        rel = (jnp.concatenate([tgt_loc, tgt_oth]) - me * vocab).astype(jnp.float32)
        tok = jnp.broadcast_to(jnp.stack([lp, coef, rel])[:, None, :], (3, SUB, tokens)).reshape(3 * SUB, tokens)

        dw_shape = jax.ShapeDtypeStruct((vocab, width), jnp.float32)
        second = steps - FIRST
        dw_t, x, g_own = pl.pallas_call(
            functools.partial(first_kernel, vocab),
            grid=(steps,),
            in_specs=[full((own, width)), full((own, width)), full((width, own)), full((width, own)),
                      pl.BlockSpec((BLOCK_V, width), lambda i: (i, 0)), full((3 * SUB, tokens))],
            out_specs=[pl.BlockSpec((BLOCK_V, width), lambda i: (jnp.minimum(i, FIRST - 1), 0)), full((width + SUB, own)),
                       pl.BlockSpec((BLOCK_V, own), lambda i: (jnp.maximum(i - FIRST, 0), 0))],
            out_shape=[dw_shape, jax.ShapeDtypeStruct((width + SUB, own), jnp.float32), jax.ShapeDtypeStruct((second * BLOCK_V, own), jnp.bfloat16)],
            scratch_shapes=[pltpu.VMEM((BLOCK_V, width), jnp.bfloat16), pltpu.VMEM((BLOCK_V, own), jnp.bfloat16), pltpu.VMEM((BLOCK_V, own), jnp.bfloat16)],
            compiler_params=params,
            cost_estimate=pl.CostEstimate(flops=unit * (2 * steps + 3 * FIRST) // steps, bytes_accessed=4 * width * vocab, transcendentals=2 * own * vocab),
            name='grads_first',
        )(hn_own, hn_oth, hnt_own, hnt_oth, w_t, tok)

        hr = h_own * r_own
        ds_part = jnp.sum(x[:width] * hr.T, axis=1)
        zt_part = wt_loc * jnp.sum(x[width:], axis=0)
        extra = jnp.stack([jnp.concatenate([ds_part, jnp.zeros((own - width,), jnp.float32)]), zt_part])
        x = x.at[width:width + 2].set(extra)
        x = lax.psum(x, 'vp')

        dw_t = pl.pallas_call(
            functools.partial(second_kernel, vocab),
            grid=(second,),
            in_specs=[full((own, width)), full((own, width)), full((width, own)),
                      pl.BlockSpec((BLOCK_V, width), lambda i: (i + FIRST, 0)), full((3 * SUB, tokens)),
                      pl.BlockSpec((BLOCK_V, own), lambda i: (i, 0)), pl.BlockSpec(memory_space=pl.ANY)],
            out_specs=pl.BlockSpec((BLOCK_V, width), lambda i: (i + FIRST, 0)),
            out_shape=dw_shape,
            scratch_shapes=[pltpu.VMEM((BLOCK_V, width), jnp.bfloat16), pltpu.VMEM((BLOCK_V, own), jnp.bfloat16)],
            input_output_aliases={6: 0},
            compiler_params=params,
            cost_estimate=pl.CostEstimate(flops=unit * 3 * second // steps, bytes_accessed=4 * width * vocab, transcendentals=own * vocab),
            name='grads_second',
        )(hn_own, hn_oth, hnt_oth, w_t, tok, g_own, dw_t)

        mine = x[width:width + 2]
        both = mine + lax.ppermute(mine, 'dp', swap_dp)
        dhn = x[:width].T
        a = jnp.sum(dhn * norm_scale * h_own, axis=-1, keepdims=True)
        dh = r_own * norm_scale * dhn - h_own * (r_own * r_own * r_own) * (a / width)
        log_sum = jnp.sum(wt_loc * log_own) + jnp.sum(wt_oth * log_oth)
        loss = (log_sum - jnp.sum(both[1])) / w_total
        return loss, dh.astype(jnp.bfloat16), dw_t.T, both[0, :width]

    return jax.shard_map(local, mesh=mesh, in_specs=(P('dp', None), P(None), P(None, 'vp'), P('dp'), P('dp')), out_specs=(P(), P('dp', None), P(None, 'vp'), P(None)), check_vma=False)
```

time: 1740 us -> 317 us (0.18)
  waiting for transfers between devices: 1370 us -> 0.05 us
  Pallas kernels: 0 us -> 252 us
  matrix products: 156 us -> 0 us
  other arithmetic: 110 us -> 15.7 us
  local copies, waits for them, and re-layouts: 42.8 us -> 10.6 us
  blocking collectives: 38.8 us -> 13.3 us
    psum x2 -> x1, waiting for transfers between devices: 1370 us -> 0.02 us  [local(): x = lax.psum(x, 'vp')]
    pallas_call x0 -> x3, Pallas kernels: none -> 252 us  [the longest x1 146 us: local(): pl.pallas_call(functools.partial(first_kernel, vocab), grid=(steps,), in_...]
    dot_general x3 -> x0, matrix products: 156 us -> none  [the longest x1 58 us: local(): logits = jnp.dot(h_norm, w_loc, preferred_element_type=jnp.float32)]
    convert_element_type x2 -> x5, other arithmetic: 64.9 us -> 5.5 us  [the longest x1 1.57 us: local(): h_own = h_loc.astype(jnp.float32)]
    unnamed x13 -> x16, local copies, waits for them, and re-layouts: 42.8 us -> 3.79 us
    reduce_sum x4 -> x8, other arithmetic: 44.4 us -> 6.36 us  [the longest x1 1.95 us: local(): a = jnp.sum(dhn * norm_scale * h_own, axis=-1, keepdims=True)]
    psum x3 -> x0, blocking collectives: 23.4 us -> none  [the longest x1 12.1 us: local(): lax.psum(jnp.sum(jnp.where(is_target, logits, 0.0), axis=-1), 'vp')]
  transfers between devices with their start and end apart: 2 -> 5, of which waited for: 1 -> 0; matrix products, arithmetic and copies ran while one was open for 3% -> 4% of each run, Pallas kernels for 0% -> 33%
where the time goes in v1:
time: 317 us; the launch traced here: 316 us
  Pallas kernels  252 us (79%)
  between operations  18.5 us (6%)
  other arithmetic  15.7 us (5%)
  blocking collectives  13.3 us (4%)
  local copies, waits for them, and re-layouts  10.6 us (3%)
  starting transfers between devices  5.92 us (2%)
    pallas_call x1, Pallas kernels, local(): pl.pallas_call(functools.partial(first_kernel, vocab), grid=(steps,), in_...  146 us
    pallas_call x1, Pallas kernels, local(): pl.pallas_call(functools.partial(second_kernel, vocab), grid=(second,), i...  55.3 us
    pallas_call x1, Pallas kernels, local(): pl.pallas_call(functools.partial(stats_kernel, vocab), grid=(steps,), in_...  50.3 us
    all_gather x1, blocking collectives, local(): stats = lax.all_gather(st, ('dp', 'vp')).reshape(dp, vp, 2, own)  13.3 us
  transfers between devices with their start and end apart: 5, of which 0 were waited for; matrix products, arithmetic and copies ran while one was open for 4% of the time, Pallas kernels for 33%

profile of v1, /device:TPU:0, one launch (start us, length us, event | category | flops | bytes accessed | tf_op | source)
XLA Modules:
  0.0 315.8 jit_solution(9157862416415733700)
XLA Ops:
  7.2 0.0 copy-start.6
  7.2 0.0 copy-start.3
  7.2 0.0 all-reduce.3.cloned.1.call-start
  7.2 1.5 copy.17
  8.7 0.0 copy-start.1
  8.7 1.6 convert_element_type.22
  10.3 3.3 %collective-permute-start = (f32[1024,512]{0,1:T(8,128)}, f32[1024,512]{0,1:T(8,128)S(1)}, u32[]{:S(2)}, u32[]{:S(2)}) collective-permute-start(f32[1024,512]{0,1:T(8,128)} %convert_element_type.22), channel_id=1, source_target_pairs={{0,8},{8,0},{1,9},{9,1},{2,10},{10,2},{3,11},{11,3},{4,12},{12,4},... | collective-permute-start | bytes 6291464 | tf_op jit(solution)/shard_map/ppermute | solution.py:132
  13.6 0.0 copy-done.6
  13.6 0.0 collective-permute-start.1
  13.6 0.0 copy-done.3
  13.6 2.0 collective-permute-start.2
  15.7 0.2 multiply_reduce_fusion.2
  15.9 0.6 multiply_multiply_fusion
  16.5 0.0 copy-done.1
  16.5 1.2 fusion.10.hnt_ref.hnt_a_ref
  17.7 50.3 %stats.1 = f32[2,1024]{1,0:T(2,128)} custom-call(bf16[512,1024]{1,0:T(8,128)(2,1)} %fusion.10.hnt_ref.hnt_a_ref, bf16[31264,512]{1,0:T(8,128)(2,1)} %bitcast.42), custom_call_target="tpu_custom_call" | custom-call | flops 32782680064 | bytes 32014336 | tf_op jit(solution)/shard_map/stats/pallas_call | solution.py:145
  68.1 1.3 multiply_convert_fusion.1
  69.3 2.3 copy.19.hn_a_ref
  71.6 0.0 collective-permute-done.1
  71.6 0.0 collective-permute-done.2
  71.6 0.0 collective-permute-done
  71.6 0.2 multiply_reduce_fusion.1
  71.8 1.2 multiply_convert_fusion
  73.0 0.0 copy-start.5
  73.0 1.2 fusion.9.hnt_b_ref
  74.2 0.0 copy-done.5
  74.2 13.3 %all-gather.1 = f32[16,2,1024]{2,1,0:T(2,128)S(1)} all-gather(f32[1,2,1024]{2,1,0:T(2,128)S(1)} %bitcast.52), channel_id=2, replica_groups=mesh['dp'=2,'vp'=8] {'dp','vp'}, dimensions={0}, use_global_device_ids=true | all-gather | bytes 139264 | tf_op jit(solution)/shard_map/all_gather | solution.py:157
  87.5 0.1 fusion.8
  87.6 0.1 fusion.4
  87.7 2.3 copy.20.hn_b_ref
  90.0 0.6 fusion.6
  92.0 0.7 broadcast_bitcast_fusion.tok_ref
  92.7 146.2 %grads_first.1 = (f32[31264,512]{1,0:T(8,128)}, f32[520,1024]{1,0:T(8,128)}, bf16[14592,1024]{1,0:T(8,128)(2,1)}) custom-call(bf16[1024,512]{1,0:T(8,128)(2,1)} %copy.19.hn_a_ref, bf16[1024,512]{1,0:T(8,128)(2,1)} %copy.20.hn_b_ref, bf16[512,1024]{1,0:T(8,128)(2,1)} %fusion.10.hnt_ref.hnt_a_ref, bf16[512,1024]{1,0:T(8,128)(2,1)} %fusion.9.hnt_b_ref, ...), custom_call_target="tpu_custom_call" | custom-call | flops 118337478656 | bytes 64028672 | tf_op jit(solution)/shard_map/grads_first/pallas_call | solution.py:173
  238.9 0.8 slice_reduce_fusion
  239.7 1.9 fusion
  241.6 0.6 maximum_dynamic-update-slice_fusion
  242.2 0.0 all-reduce.3.cloned.1.call-update
  242.3 0.0 copy-start.2
  242.3 55.3 %grads_second.1 = f32[31264,512]{1,0:T(8,128)} custom-call(bf16[1024,512]{1,0:T(8,128)(2,1)} %copy.19.hn_a_ref, bf16[1024,512]{1,0:T(8,128)(2,1)} %copy.20.hn_b_ref, bf16[512,1024]{1,0:T(8,128)(2,1)} %fusion.9.hnt_b_ref, bf16[31264,512]{1,0:T(8,128)(2,1)} %bitcast.44, f32[24,2048]{1,0:T(8,128)} %broadcast_bitcast_fusion.tok_ref, ...), custom_call_target="tpu_custom_call", output_to_operand_aliasing={{}: (6, {})} | custom-call | flops 45575921664 | bytes 64028672 | tf_op jit(solution)/shard_map/grads_second/pallas_call | solution.py:194
  297.6 0.0 copy-start.4
  298.8 0.0 all-reduce.3.cloned.1.call-done
  298.8 0.0 copy-start
  298.8 0.9 slice.52
  299.7 0.5 collective-permute-start.3
  300.3 0.0 copy-done.2
  300.3 1.9 multiply_reduce_fusion
  302.2 0.0 copy-done.4
  302.2 0.0 copy-done
  302.2 1.5 subtract_convert_fusion
  303.7 2.3 copy.23
  306.0 0.0 collective-permute-done.3
  306.0 0.6 slice_reduce_fusion.1
  306.6 0.6 slice.55
  (10 shorter events, 0.1 us)
Async XLA Ops:
  7.2 6.5 %copy-start.6 = (s32[1024]{0:T(1024)S(1)}, s32[1024]{0:T(1024)}, u32[]{:S(2)}) copy-start(s32[1024]{0:T(1024)} %param.10) | copy-start | bytes 12292
  7.2 6.5 %copy-start.3 = (f32[1024]{0:T(1024)S(1)}, f32[1024]{0:T(1024)}, u32[]{:S(2)}) copy-start(f32[1024]{0:T(1024)} %param.11) | copy-start | bytes 12292
  7.2 291.6 %all-reduce.3.cloned.1.call-start = ((), (), s32[]{:S(2)}) async-start(), calls=%async_computation | async-start | bytes 4259840 | tf_op jit(solution)/shard_map/psum | solution.py:192
  8.7 7.8 %copy-start.1 = (f32[512]{0:T(512)S(1)}, f32[512]{0:T(512)}, u32[]{:S(2)}) copy-start(f32[512]{0:T(512)} %param.8) | copy-start | bytes 6148
  10.3 61.3 %collective-permute-start = (f32[1024,512]{0,1:T(8,128)}, f32[1024,512]{0,1:T(8,128)S(1)}, u32[]{:S(2)}, u32[]{:S(2)}) collective-permute-start(f32[1024,512]{0,1:T(8,128)} %convert_element_type.22), channel_id=1, source_target_pairs={{0,8},{8,0},{1,9},{9,1},{2,10},{10,2},{3,11},{11,3},{4,12},{12,4},... | collective-permute-start | bytes 6291464 | tf_op jit(solution)/shard_map/ppermute | solution.py:132
  13.6 58.0 %collective-permute-start.1 = (s32[1024]{0:T(1024)S(1)}, s32[1024]{0:T(1024)S(1)}, u32[]{:S(2)}, u32[]{:S(2)}) collective-permute-start(s32[1024]{0:T(1024)S(1)} %copy-done.6), channel_id=1, source_target_pairs={{0,8},{8,0},{1,9},{9,1},{2,10},{10,2},{3,11},{11,3},{4,12},{12,4},... | collective-permute-start | bytes 12296 | tf_op jit(solution)/shard_map/ppermute | solution.py:133
  13.6 58.0 %collective-permute-start.2 = (f32[1024]{0:T(1024)S(1)}, f32[1024]{0:T(1024)S(1)}, u32[]{:S(2)}, u32[]{:S(2)}) collective-permute-start(f32[1024]{0:T(1024)S(1)} %copy-done.3), channel_id=1, source_target_pairs={{0,8},{8,0},{1,9},{9,1},{2,10},{10,2},{3,11},{11,3},{4,12},{12,4},... | collective-permute-start | bytes 12296 | tf_op jit(solution)/shard_map/ppermute | solution.py:134
  73.0 1.2 copy-start.5
  242.3 58.0 %copy-start.2 = (f32[512]{0:T(512)S(1)}, f32[512]{0:T(512)}, u32[]{:S(2)}) copy-start(f32[512]{0:T(512)} %param.8) | copy-start | bytes 6148
  297.6 4.7 %copy-start.4 = (f32[1024]{0:T(1024)S(1)}, f32[1024]{0:T(1024)}, u32[]{:S(2)}) copy-start(f32[1024]{0:T(1024)} %get-tuple-element.49) | copy-start | bytes 12292
  298.8 3.4 %copy-start = (f32[520,1024]{1,0:T(8,128)S(1)}, f32[520,1024]{1,0:T(8,128)}, u32[]{:S(2)}) copy-start(f32[520,1024]{1,0:T(8,128)} %all-reduce.3.cloned.1.call-done) | copy-start | bytes 6389764
  299.7 6.3 %collective-permute-start.3 = (f32[2,1024]{1,0:T(2,128)S(1)}, f32[2,1024]{1,0:T(2,128)S(1)}, u32[]{:S(2)}, u32[]{:S(2)}) collective-permute-start(f32[2,1024]{1,0:T(2,128)S(1)} %slice.52), channel_id=1, source_target_pairs={{0,8},{8,0},{1,9},{9,1},{2,10},{10,2},{3,11},{11,3},{4,12},{12,4},... | collective-permute-start | bytes 24584 | tf_op jit(solution)/shard_map/ppermute | solution.py:210
Sparse Core Ops, SparseCore 0:
  242.4 53.0 all-reduce.2

commit v2 on v1

v2 whole, which is shorter than its diff:
```python
import functools

import jax
import jax.numpy as jnp
from jax import lax
from jax.experimental import pallas as pl
from jax.experimental.pallas import tpu as pltpu
from jax.sharding import PartitionSpec as P

EPS = 1e-6
SUB = 8
BLOCK_V = 1536
CHUNK = 512
GCHUNK = 512
MAX_SUM = 1e18
TN = (((0,), (0,)), ((), ()))
NT = (((1,), (1,)), ((), ()))


def last_rows(vocab):
    return vocab - (vocab - 1) // BLOCK_V * BLOCK_V


def stats_kernel(vocab, hnt_ref, w_ref, out_ref, z_ref, m_ref, s_ref, s_new_ref):
    i = pl.program_id(0)
    last = pl.num_programs(0) - 1
    tokens = hnt_ref.shape[1]

    @pl.when(i == 0)
    def _():
        z = jnp.dot(w_ref[:CHUNK, :], hnt_ref[...], preferred_element_type=jnp.float32)
        m_ref[...] = jnp.broadcast_to(jnp.max(z, axis=0, keepdims=True), m_ref.shape)
        s_ref[...] = jnp.zeros(s_ref.shape, jnp.float32)

    def exact(rows):
        for c in range(0, tokens, CHUNK):
            cols = pl.ds(c, CHUNK)
            z = jnp.dot(w_ref[:rows, :], hnt_ref[:, cols], preferred_element_type=jnp.float32)
            z = z.reshape(rows // SUB, SUB, CHUNK)
            m_old = m_ref[:, cols]
            m_new = jnp.maximum(m_old, jnp.max(z, axis=0))
            s_ref[:, cols] = s_ref[:, cols] * jnp.exp(m_old - m_new) + jnp.sum(jnp.exp(z - m_new[None]), axis=0)
            m_ref[:, cols] = m_new

    @pl.when(i < last)
    def _():
        largest = []
        for c in range(0, tokens, CHUNK):
            cols = pl.ds(c, CHUNK)
            z = jnp.dot(w_ref[...], hnt_ref[:, cols], preferred_element_type=jnp.float32)
            z_ref[:, cols] = z
            shifted = z.reshape(BLOCK_V // SUB, SUB, CHUNK) - m_ref[:, cols][None]
            total = s_ref[:, cols] + jnp.sum(jnp.exp(shifted), axis=0)
            largest.append(jnp.max(total))
            s_new_ref[:, cols] = total
        safe = functools.reduce(jnp.maximum, largest) <= MAX_SUM

        @pl.when(safe)
        def _():
            s_ref[...] = s_new_ref[...]

        @pl.when(jnp.logical_not(safe))
        def _():
            exact(BLOCK_V)

    @pl.when(i == last)
    def _():
        exact(last_rows(vocab))
        top = jnp.max(m_ref[...], axis=0, keepdims=True)
        out_ref[0:1, :] = top
        out_ref[1:2, :] = jnp.sum(s_ref[...] * jnp.exp(m_ref[...] - top), axis=0, keepdims=True)


def softmax_grad(z, step, tok_ref, toks):
    shape = (z.shape[0] // SUB, SUB, z.shape[1])
    z = z.reshape(shape)
    first_row = (lax.broadcasted_iota(jnp.int32, shape, 0) * SUB).astype(jnp.float32)
    row0 = (lax.broadcasted_iota(jnp.int32, shape[1:], 0) + step * BLOCK_V).astype(jnp.float32)
    hit = (tok_ref[2 * SUB:, toks] - row0)[None] == first_row
    g = jnp.exp(z - tok_ref[:SUB, toks][None]) - jnp.where(hit, tok_ref[SUB:2 * SUB, toks][None], 0.0)
    picked = jnp.sum(jnp.where(hit, z, 0.0), axis=0)
    return g.reshape(shape[0] * SUB, shape[2]).astype(jnp.bfloat16), picked


def other_grad(step, rows, w_ref, hnt_ref, tok_ref, g_ref):
    own = hnt_ref.shape[1]
    for c in range(0, own, GCHUNK):
        cols = pl.ds(c, GCHUNK)
        z = jnp.dot(w_ref[:rows, :], hnt_ref[:, cols], preferred_element_type=jnp.float32)
        g_ref[:rows, cols] = softmax_grad(z, step, tok_ref, pl.ds(own + c, GCHUNK))[0]


def weight_grad(rows, ga_ref, gb_ref, hnt_a_ref, hnt_b_ref):
    return (lax.dot_general(ga_ref[:rows, :], hnt_a_ref[...], NT, preferred_element_type=jnp.float32)
            + lax.dot_general(gb_ref[:rows, :], hnt_b_ref[...], NT, preferred_element_type=jnp.float32))


def first_kernel(vocab, first, hnt_a_ref, hnt_b_ref, w_ref, z_ref, tok_ref, dw_ref, x_ref, g_out_ref, ga_ref, gb_ref):
    i = pl.program_id(0)
    last = pl.num_programs(0) - 1
    width, own = hnt_a_ref.shape

    @pl.when(i == 0)
    def _():
        x_ref[...] = jnp.zeros(x_ref.shape, jnp.float32)

    def own_part(rows, g_ref, saved=False):
        for c in range(0, own, GCHUNK):
            cols = pl.ds(c, GCHUNK)
            z = z_ref[:, cols] if saved else jnp.dot(w_ref[:rows, :], hnt_a_ref[:, cols], preferred_element_type=jnp.float32)
            g, picked = softmax_grad(z, i, tok_ref, cols)
            g_ref[:rows, cols] = g
            x_ref[width:, cols] += picked
            x_ref[:width, cols] += lax.dot_general(w_ref[:rows, :], g, TN, preferred_element_type=jnp.float32)

    @pl.when(i < first)
    def _():
        own_part(BLOCK_V, ga_ref, saved=True)
        other_grad(i, BLOCK_V, w_ref, hnt_b_ref, tok_ref, gb_ref)
        dw_ref[...] = weight_grad(BLOCK_V, ga_ref, gb_ref, hnt_a_ref, hnt_b_ref)

    @pl.when(jnp.logical_and(i >= first, i < last))
    def _():
        own_part(BLOCK_V, g_out_ref)

    @pl.when(i == last)
    def _():
        own_part(last_rows(vocab), g_out_ref)


def second_kernel(vocab, first, hnt_a_ref, hnt_b_ref, w_ref, tok_ref, ga_ref, dw_in_ref, dw_ref, gb_ref):
    i = pl.program_id(0)
    last = pl.num_programs(0) - 1

    def block(rows):
        other_grad(i + first, rows, w_ref, hnt_b_ref, tok_ref, gb_ref)
        dw_ref[:rows, :] = weight_grad(rows, ga_ref, gb_ref, hnt_a_ref, hnt_b_ref)

    @pl.when(i < last)
    def _():
        block(BLOCK_V)

    @pl.when(i == last)
    def _():
        block(last_rows(vocab))


def hidden_grad_kernel(x_ref, h_ref, scale_ref, dh_ref):
    width = h_ref.shape[1]
    h = h_ref[...].astype(jnp.float32)
    r = lax.rsqrt(jnp.mean(h * h, axis=-1, keepdims=True) + EPS)
    sd = scale_ref[...] * x_ref[:width, :].T
    a = jnp.sum(sd * h, axis=-1, keepdims=True)
    dh_ref[...] = (r * sd - h * (r * r * r) * (a / width)).astype(jnp.bfloat16)


def full(shape):
    return pl.BlockSpec(shape, lambda i: (0,) * len(shape))


def solution(mesh):
    dp, vp = mesh.shape['dp'], mesh.shape['vp']

    def local(h_loc, norm_scale, w_loc, tgt_loc, wt_loc):
        own, width = h_loc.shape
        vocab = w_loc.shape[1]
        tokens = dp * own
        steps = pl.cdiv(vocab, BLOCK_V)
        first = (steps + 1) // 2
        second = steps - first
        me = lax.axis_index('vp')
        my_dp = lax.axis_index('dp')
        swap_dp = [(0, 1), (1, 0)]
        w_t = w_loc.T

        scale = norm_scale[None, :]
        whole = pltpu.CompilerParams(vmem_limit_bytes=40 * 2**20)
        h_own = h_loc.astype(jnp.float32)
        h_oth = lax.ppermute(h_own, 'dp', swap_dp)
        tgt_oth = lax.ppermute(tgt_loc, 'dp', swap_dp)
        wt_oth = lax.ppermute(wt_loc, 'dp', swap_dp)

        def rstd(h):
            return lax.rsqrt(jnp.mean(h * h, axis=-1, keepdims=True) + EPS)

        hr_own = h_own * rstd(h_own)
        hnt_own = (hr_own * norm_scale).astype(jnp.bfloat16).T

        params = pltpu.CompilerParams(dimension_semantics=('arbitrary',), vmem_limit_bytes=60 * 2**20)
        unit = 2 * own * width * vocab
        st, z_own = pl.pallas_call(
            functools.partial(stats_kernel, vocab),
            grid=(steps,),
            in_specs=[full((width, own)), pl.BlockSpec((BLOCK_V, width), lambda i: (i, 0))],
            out_specs=[full((2, own)), pl.BlockSpec((BLOCK_V, own), lambda i: (jnp.minimum(i, first), 0))],
            out_shape=[jax.ShapeDtypeStruct((2, own), jnp.float32), jax.ShapeDtypeStruct(((first + 1) * BLOCK_V, own), jnp.float32)],
            scratch_shapes=[pltpu.VMEM((SUB, own), jnp.float32)] * 3,
            compiler_params=params,
            cost_estimate=pl.CostEstimate(flops=unit, bytes_accessed=(2 * width + 2 * own) * vocab, transcendentals=own * vocab),
            name='stats',
        )(hnt_own, w_t)
        h_oth, tgt_oth, wt_oth, st = lax.optimization_barrier((h_oth, tgt_oth, wt_oth, st))
        stats = lax.all_gather(st, ('dp', 'vp')).reshape(dp, vp, 2, own)
        top = jnp.max(stats[:, :, 0], axis=1)
        log_norm = top + jnp.log(jnp.sum(stats[:, :, 1] * jnp.exp(stats[:, :, 0] - top[:, None]), axis=1))
        w_total = jnp.sum(wt_loc) + jnp.sum(wt_oth)
        log_own = lax.dynamic_index_in_dim(log_norm, my_dp, 0, keepdims=False)
        log_oth = lax.dynamic_index_in_dim(log_norm, 1 - my_dp, 0, keepdims=False)

        hn_oth = (h_oth * rstd(h_oth) * norm_scale).astype(jnp.bfloat16)
        hnt_oth = hn_oth.T
        coef = jnp.concatenate([wt_loc, wt_oth]) / w_total
        lp = jnp.concatenate([log_own, log_oth]) - jnp.log(coef)
        rel = jnp.concatenate([tgt_loc, tgt_oth]) - me * vocab
        rel = jnp.where(rel < vocab, rel, -1).astype(jnp.float32)
        tok = jnp.broadcast_to(jnp.stack([lp, coef, rel])[:, None, :], (3, SUB, tokens)).reshape(3 * SUB, tokens)

        dw_shape = jax.ShapeDtypeStruct((vocab, width), jnp.float32)
        dw_t, x, g_own = pl.pallas_call(
            functools.partial(first_kernel, vocab, first),
            grid=(steps,),
            in_specs=[full((width, own)), full((width, own)), pl.BlockSpec((BLOCK_V, width), lambda i: (i, 0)),
                      pl.BlockSpec((BLOCK_V, own), lambda i: (jnp.minimum(i, first - 1), 0)), full((3 * SUB, tokens))],
            out_specs=[pl.BlockSpec((BLOCK_V, width), lambda i: (jnp.minimum(i, first - 1), 0)), full((width + SUB, own)),
                       pl.BlockSpec((BLOCK_V, own), lambda i: (jnp.maximum(i - first, 0), 0))],
            out_shape=[dw_shape, jax.ShapeDtypeStruct((width + SUB, own), jnp.float32), jax.ShapeDtypeStruct((second * BLOCK_V, own), jnp.bfloat16)],
            scratch_shapes=[pltpu.VMEM((BLOCK_V, own), jnp.bfloat16)] * 2,
            compiler_params=params,
            cost_estimate=pl.CostEstimate(flops=unit * (2 * steps + 2 * first) // steps, bytes_accessed=(4 * width + 2 * own) * vocab, transcendentals=2 * own * vocab),
            name='grads_first',
        )(hnt_own, hnt_oth, w_t, z_own, tok)

        ds_part = jnp.sum(x[:width] * hr_own.T, axis=1)
        zt_part = wt_loc * jnp.sum(x[width:], axis=0)
        extra = jnp.stack([jnp.concatenate([ds_part, jnp.zeros((own - width,), jnp.float32)]), zt_part])
        x = x.at[width:width + 2].set(extra)
        x = lax.psum(x, 'vp')

        dw_t = pl.pallas_call(
            functools.partial(second_kernel, vocab, first),
            grid=(second,),
            in_specs=[full((width, own)), full((width, own)),
                      pl.BlockSpec((BLOCK_V, width), lambda i: (i + first, 0)), full((3 * SUB, tokens)),
                      pl.BlockSpec((BLOCK_V, own), lambda i: (i, 0)), pl.BlockSpec(memory_space=pl.ANY)],
            out_specs=pl.BlockSpec((BLOCK_V, width), lambda i: (i + first, 0)),
            out_shape=dw_shape,
            scratch_shapes=[pltpu.VMEM((BLOCK_V, own), jnp.bfloat16)],
            input_output_aliases={5: 0},
            compiler_params=params,
            cost_estimate=pl.CostEstimate(flops=unit * 3 * second // steps, bytes_accessed=4 * width * vocab, transcendentals=own * vocab),
            name='grads_second',
        )(hnt_own, hnt_oth, w_t, tok, g_own, dw_t)

        x, dw_t = lax.optimization_barrier((x, dw_t))
        mine = x[width:width + 2]
        both = mine + lax.ppermute(mine, 'dp', swap_dp)
        dh = pl.pallas_call(
            hidden_grad_kernel,
            out_shape=jax.ShapeDtypeStruct((own, width), jnp.bfloat16),
            compiler_params=whole,
            name='hidden_grad',
        )(x, h_loc, scale)
        log_sum = jnp.sum(wt_loc * log_own) + jnp.sum(wt_oth * log_oth)
        loss = (log_sum - jnp.sum(both[1])) / w_total
        return loss, dh, dw_t.T, both[0, :width]

    return jax.shard_map(local, mesh=mesh, in_specs=(P('dp', None), P(None), P(None, 'vp'), P('dp'), P('dp')), out_specs=(P(), P('dp', None), P(None, 'vp'), P(None)), check_vma=False)
```

time: 317 us -> 293 us (0.924)
  Pallas kernels: 252 us -> 240 us
  other arithmetic: 15.7 us -> 9.31 us
  local copies, waits for them, and re-layouts: 10.6 us -> 5.16 us
    pallas_call x2 -> x3, Pallas kernels: 201 us -> 187 us  [the longest x1 128 us: local(): pl.pallas_call(functools.partial(first_kernel, vocab, first), grid=(steps...]
    convert_element_type x2 -> x0, local copies, waits for them, and re-layouts: 4.57 us -> none  [the longest x1 2.28 us: local(): hn_oth = (h_oth * rstd(h_oth) * norm_scale).astype(jnp.bfloat16)]
    convert_element_type x4 -> x1, other arithmetic: 3.93 us -> 0.02 us  [local(): rel = jnp.where(rel < vocab, rel, -1).astype(jnp.float32)]
    ppermute x1, starting transfers between devices: 0.02 us -> 3.35 us  [local(): tgt_oth = lax.ppermute(tgt_loc, 'dp', swap_dp)]
  transfers between devices with their start and end apart: 5 -> 5, of which waited for: 0 -> 0; matrix products, arithmetic and copies ran while one was open for 4% -> 2% of each run, Pallas kernels for 33% -> 38%
where the time goes in v2:
time: 293 us; the launch traced here: 292 us
  Pallas kernels  240 us (82%)
  between operations  18.5 us (6%)
  blocking collectives  12.8 us (4%)
  other arithmetic  9.31 us (3%)
  starting transfers between devices  6.2 us (2%)
  local copies, waits for them, and re-layouts  5.16 us (2%)
    pallas_call x1, Pallas kernels, local(): pl.pallas_call(functools.partial(first_kernel, vocab, first), grid=(steps...  128 us
    pallas_call x1, Pallas kernels, local(): pl.pallas_call(functools.partial(second_kernel, vocab, first), grid=(seco...  57.1 us
    pallas_call x1, Pallas kernels, local(): pl.pallas_call(functools.partial(stats_kernel, vocab), grid=(steps,), in_...  52.8 us
    all_gather x1, blocking collectives, local(): stats = lax.all_gather(st, ('dp', 'vp')).reshape(dp, vp, 2, own)  12.8 us
  transfers between devices with their start and end apart: 5, of which 0 were waited for; matrix products, arithmetic and copies ran while one was open for 2% of the time, Pallas kernels for 38%

profile of v2, /device:TPU:0, one launch (start us, length us, event | category | flops | bytes accessed | tf_op | source)
XLA Modules:
  0.0 291.9 jit_solution(13779191710463492283)
XLA Ops:
  7.2 0.0 all-reduce.3.cloned.1.call-start
  7.2 3.3 %collective-permute-start.1 = (s32[1024]{0:T(1024)}, s32[1024]{0:T(1024)S(1)}, u32[]{:S(2)}, u32[]{:S(2)}) collective-permute-start(s32[1024]{0:T(1024)} %param.10), channel_id=1, source_target_pairs={{0,8},{8,0},{1,9},{9,1},{2,10},{10,2},{3,11},{11,3},{4,12},{12,4},... | collective-permute-start | bytes 12296 | tf_op jit(solution)/shard_map/ppermute | solution.py:180
  10.6 0.1 collective-permute-start.2
  10.6 1.5 copy.12
  12.1 0.0 copy-start.2
  12.1 1.6 convert_element_type.19
  13.7 2.0 collective-permute-start
  15.7 0.2 multiply_reduce_fusion.1
  15.9 0.0 copy-done.2
  15.9 1.2 fusion.1.hnt_ref.hnt_a_ref
  17.2 52.8 %stats.1 = (f32[2,1024]{1,0:T(2,128)}, f32[18432,1024]{1,0:T(8,128)}) custom-call(bf16[512,1024]{1,0:T(8,128)(2,1)} %fusion.1.hnt_ref.hnt_a_ref, bf16[31264,512]{1,0:T(8,128)(2,1)} %bitcast.38), custom_call_target="tpu_custom_call" | custom-call | flops 32782680064 | bytes 96043008 | tf_op jit(solution)/shard_map/stats/pallas_call | solution.py:191
  70.0 0.0 collective-permute-done.1
  70.0 0.0 collective-permute-done.2
  70.0 0.0 collective-permute-done
  70.0 0.2 multiply_reduce_fusion
  70.2 0.0 copy-start.5
  70.2 0.0 copy-start.4
  70.2 0.0 copy-start.6
  70.2 1.2 fusion.2.hnt_b_ref
  71.4 0.0 copy-done.5
  71.4 12.8 %all-gather.1 = f32[16,2,1024]{2,1,0:T(2,128)S(1)} all-gather(f32[1,2,1024]{2,1,0:T(2,128)S(1)} %bitcast.48), channel_id=2, replica_groups=mesh['dp'=2,'vp'=8] {'dp','vp'}, dimensions={0}, use_global_device_ids=true | all-gather | bytes 139264 | tf_op jit(solution)/shard_map/all_gather | solution.py:203
  84.2 0.1 fusion.10
  84.4 0.1 fusion.6
  84.5 0.0 copy-done.4
  84.5 0.6 fusion.8
  86.4 0.0 copy-done.6
  86.5 0.7 broadcast_bitcast_fusion.tok_ref
  87.2 127.7 %grads_first.1 = (f32[31264,512]{1,0:T(8,128)}, f32[520,1024]{1,0:T(8,128)}, bf16[15360,1024]{1,0:T(8,128)(2,1)}) custom-call(bf16[512,1024]{1,0:T(8,128)(2,1)} %fusion.1.hnt_ref.hnt_a_ref, bf16[512,1024]{1,0:T(8,128)(2,1)} %fusion.2.hnt_b_ref, bf16[31264,512]{1,0:T(8,128)(2,1)} %bitcast.39, f32[18432,1024]{1,0:T(8,128)} %get-tuple-element.31.z_ref, ...), custom_call_target="tpu_custom_call" | custom-call | flops 99909124096 | bytes 128057344 | tf_op jit(solution)/shard_map/grads_first/pallas_call | solution.py:219
  214.9 2.0 fusion
  216.9 0.8 slice_reduce_fusion
  217.7 0.6 maximum_dynamic-update-slice_fusion
  218.3 0.0 all-reduce.3.cloned.1.call-update
  218.3 0.0 copy-start
  218.3 0.0 copy-start.3
  218.3 57.1 %grads_second.1 = f32[31264,512]{1,0:T(8,128)} custom-call(bf16[512,1024]{1,0:T(8,128)(2,1)} %fusion.1.hnt_ref.hnt_a_ref, bf16[512,1024]{1,0:T(8,128)(2,1)} %fusion.2.hnt_b_ref, bf16[31264,512]{1,0:T(8,128)(2,1)} %bitcast.40, f32[24,2048]{1,0:T(8,128)} %broadcast_bitcast_fusion.tok_ref, ...), custom_call_target="tpu_custom_call", output_to_operand_aliasing={{}: (5, {})} | custom-call | flops 46832398336 | bytes 64028672 | tf_op jit(solution)/shard_map/grads_second/pallas_call | solution.py:239
  275.4 0.0 all-reduce.3.cloned.1.call-done.x_ref
  275.4 0.8 slice.43
  276.1 0.8 collective-permute-start.3
  278.1 0.0 copy-done
  278.2 0.0 copy-done.3
  278.2 0.0 copy-start.1
  278.2 1.6 copy-done.1
  279.8 2.3 hidden_grad.1
  282.1 0.0 collective-permute-done.3
  282.1 0.6 slice_reduce_fusion.1
  282.7 0.6 slice.49
  (10 shorter events, 0.1 us)
Async XLA Ops:
  7.2 268.2 %all-reduce.3.cloned.1.call-start = ((), (), s32[]{:S(2)}) async-start(), calls=%async_computation | async-start | bytes 4259840 | tf_op jit(solution)/shard_map/psum | solution.py:237
  7.2 62.7 %collective-permute-start.1 = (s32[1024]{0:T(1024)}, s32[1024]{0:T(1024)S(1)}, u32[]{:S(2)}, u32[]{:S(2)}) collective-permute-start(s32[1024]{0:T(1024)} %param.10), channel_id=1, source_target_pairs={{0,8},{8,0},{1,9},{9,1},{2,10},{10,2},{3,11},{11,3},{4,12},{12,4},... | collective-permute-start | bytes 12296 | tf_op jit(solution)/shard_map/ppermute | solution.py:180
  10.6 59.4 %collective-permute-start.2 = (f32[1024]{0:T(1024)}, f32[1024]{0:T(1024)S(1)}, u32[]{:S(2)}, u32[]{:S(2)}) collective-permute-start(f32[1024]{0:T(1024)} %param.11), channel_id=1, source_target_pairs={{0,8},{8,0},{1,9},{9,1},{2,10},{10,2},{3,11},{11,3},{4,12},{12,4},... | collective-permute-start | bytes 12296 | tf_op jit(solution)/shard_map/ppermute | solution.py:181
  12.1 3.8 %copy-start.2 = (f32[512]{0:T(512)S(1)}, f32[512]{0:T(512)}, u32[]{:S(2)}) copy-start(f32[512]{0:T(512)} %param.8) | copy-start | bytes 6148
  13.7 56.3 %collective-permute-start = (f32[1024,512]{0,1:T(8,128)}, f32[1024,512]{0,1:T(8,128)S(1)}, u32[]{:S(2)}, u32[]{:S(2)}) collective-permute-start(f32[1024,512]{0,1:T(8,128)} %convert_element_type.19), channel_id=1, source_target_pairs={{0,8},{8,0},{1,9},{9,1},{2,10},{10,2},{3,11},{11,3},{4,12},{12,4},... | collective-permute-start | bytes 6291464 | tf_op jit(solution)/shard_map/ppermute | solution.py:179
  70.2 1.3 copy-start.5
  70.2 14.3 %copy-start.4 = (f32[1024]{0:T(1024)S(1)}, f32[1024]{0:T(1024)}, u32[]{:S(2)}) copy-start(f32[1024]{0:T(1024)} %param.11) | copy-start | bytes 12292
  70.2 16.2 %copy-start.6 = (s32[1024]{0:T(1024)S(1)}, s32[1024]{0:T(1024)}, u32[]{:S(2)}) copy-start(s32[1024]{0:T(1024)} %param.10) | copy-start | bytes 12292
  218.3 59.9 %copy-start = (bf16[1024,512]{1,0:T(8,128)(2,1)S(1)}, bf16[1024,512]{1,0:T(8,128)(2,1)}, u32[]{:S(2)}) copy-start(bf16[1024,512]{1,0:T(8,128)(2,1)} %h_ref.1) | copy-start | bytes 3145732
  218.3 59.8 %copy-start.3 = (f32[512]{0:T(512)S(1)}, f32[512]{0:T(512)}, u32[]{:S(2)}) copy-start(f32[512]{0:T(512)} %param.8) | copy-start | bytes 6148
  276.1 5.9 %collective-permute-start.3 = (f32[2,1024]{1,0:T(2,128)S(1)}, f32[2,1024]{1,0:T(2,128)S(1)}, u32[]{:S(2)}, u32[]{:S(2)}) collective-permute-start(f32[2,1024]{1,0:T(2,128)S(1)} %slice.43), channel_id=1, source_target_pairs={{0,8},{8,0},{1,9},{9,1},{2,10},{10,2},{3,11},{11,3},{4,12},{12,4},... | collective-permute-start | bytes 24584 | tf_op jit(solution)/shard_map/ppermute | solution.py:256
  278.2 1.6 copy-start.1
Sparse Core Ops, SparseCore 0:
  218.4 53.2 all-reduce.2
